TPU v7x, 32 devices: a whole 2x2x4 slice. The times are simulated.
32 devices in a mesh: silo: 4 (over z), row: 8 (over y, x, core).
Axes of the slice: x: 2, y: 2, z: 4, core: 2. Of those that a mesh axis runs over, the one named last changes fastest.
Arguments:
- silo_grams: float32 [8, 4096, 4096], P('silo', 'row'), may hold values from -9 to 81, as said below
- silo_weights: bfloat16 [8, 4096, 640], P('silo', 'row'), may hold values from -6 to 6
Outputs:
- merged_rows: float32 [640, 4096], P(('silo', 'row'))
Inputs may be any that keep to these rules, and one draw needn't show every extreme that they name: `silo_grams`: each silo's Gram is symmetric up to float32 rounding and positive definite.
All inputs are finite; a program needn't handle non-finite values.
Results may differ from a plain program's by a relative error of at most 0.0003.
Values may be sent and summed in bfloat16 or wider, within the bound.
No kernel may reach another device: no remote copies, remote signals or barrier semaphores. Data moves between devices by JAX's collectives and lax.ppermute only.
A program may use at most 128 MiB of HBM per device.

v0:
```python
import jax
import jax.numpy as jnp
from jax import lax
from jax.sharding import PartitionSpec as P

ITERS = 2
full_precision = lax.Precision.HIGHEST


def conj_grad(right_side, apply_op, sum_squares, sum_curv):
    solution = jnp.zeros_like(right_side)
    residual = right_side
    direction = right_side
    res_norm = sum_squares(jnp.sum(residual * residual, axis=0))
    for iteration in range(ITERS):
        mapped = apply_op(direction)
        step_size = res_norm / sum_curv(jnp.sum(direction * mapped, axis=0))
        solution = solution + step_size * direction
        residual = residual - step_size * mapped
        if iteration + 1 < ITERS:
            next_norm = sum_squares(jnp.sum(residual * residual, axis=0))
            direction = residual + next_norm / res_norm * direction
            res_norm = next_norm
    return solution


def local(silo_grams, silo_weights):
    partial_op = jnp.sum(silo_grams, axis=0)
    partial_rhs = jnp.einsum(
        "srk,skc->rc",
        silo_grams,
        lax.all_gather(silo_weights, "row", axis=1, tiled=True).astype(jnp.float32),
        precision=full_precision,
    )
    operator = lax.psum(partial_op, "silo")
    right_side = lax.psum_scatter(partial_rhs, "silo", scatter_dimension=1, tiled=True)

    def apply_cols(direction):
        return jnp.dot(
            operator, lax.all_gather(direction, "row", axis=0, tiled=True), precision=full_precision
        )

    def squares_cols(values):
        return lax.psum(values, "row")

    def curv_values(values):
        return lax.psum(values, "row")

    solution = conj_grad(right_side, apply_cols, squares_cols, curv_values)
    transposed = solution.T
    return lax.all_to_all(transposed, "row", split_axis=0, concat_axis=1, tiled=True)


def solution(mesh):
    placed = (P("silo", "row", None), P("silo", "row", None))
    return jax.shard_map(
        local, mesh=mesh, in_specs=placed, out_specs=P(("silo", "row"), None), check_vma=False
    )
```

profile of v0, /device:TPU:0, one launch (start us, length us, event | category | flops | bytes accessed | tf_op | source)
XLA Modules:
  0.0 567.5 jit_solution(10931932025676428913)
XLA Ops:
  6.5 0.0 all-gather.4.cloned.1.call-start
  6.5 2.4 copy.6
  9.0 0.0 all-gather.4.cloned.1.call-update
  9.0 0.0 reduce-scatter.2.cloned.1.call-start
  9.0 68.1 %all-gather.4.cloned.1.call-done = bf16[2,4096,640]{1,2,0:T(8,128)(2,1)} async-done(((bf16[2,512,640]{1,2,0:T(8,128)(2,1)}), bf16[2,4096,640]{1,2,0:T(8,128)(2,1)}) %all-gather.4.cloned.1.call-update) | async-done | bytes 10485776 | tf_op jit(solution)/shard_map/all_gather | solution.py:32
  77.1 21.3 %convolution_bitcast_fusion = f32[512,640]{0,1:T(8,128)} fusion(f32[2,512,4096]{2,1,0:T(8,128)} %param.2, bf16[2,4096,640]{1,2,0:T(8,128)(2,1)} %all-gather.4.cloned.1.call-done), kind=kOutput, calls=%fused_computation | convolution fusion | flops 32212254720 | bytes 28573696 | tf_op jit(solution)/shard_map/srk,skc->rc/dot_general | solution.py:29
  98.4 0.0 reduce-scatter.2.cloned.1.call-update
  98.5 0.0 all-reduce.3.cloned.1.call-start
  98.5 11.6 %reduce_sum.46 = f32[512,4096]{1,0:T(8,128)} reduce(f32[2,512,4096]{2,1,0:T(8,128)} %param.2, f32[]{:T(128)} %constant.0.clone.1), dimensions={0}, to_apply=%region_3.0 | reduce | flops 2097152 | bytes 25165828 | tf_op jit(solution)/shard_map/reduce_sum | solution.py:28
  110.1 0.0 all-reduce.3.cloned.1.call-update
  110.1 0.0 all-gather.6.cloned.1.call-start
  110.2 19.8 %reduce-scatter.2.cloned.1.call-done = f32[512,160]{0,1:T(8,128)} async-done(((f32[512,640]{0,1:T(8,128)}), f32[512,160]{0,1:T(8,128)}) %reduce-scatter.2.cloned.1.call-update) | async-done | bytes 327696 | tf_op jit(solution)/shard_map/reduce_scatter | solution.py:36
  130.0 0.0 copy-start
  130.0 0.0 all-gather.6.cloned.1.call-update
  130.0 0.2 all-gather.8.cloned.1.call-start
  130.2 291.8 %all-reduce.3.cloned.1.call-done = f32[512,4096]{1,0:T(8,128)} async-done(((f32[512,4096]{1,0:T(8,128)}), f32[512,4096]{1,0:T(8,128)}) %all-reduce.3.cloned.1.call-update) | async-done | bytes 8388624 | tf_op jit(solution)/shard_map/psum | solution.py:35
  422.0 30.8 %all-gather.6.cloned.1.call-done = f32[4096,160]{0,1:T(8,128)} async-done(((f32[512,160]{0,1:T(8,128)}), f32[4096,160]{0,1:T(8,128)}) %all-gather.6.cloned.1.call-update) | async-done | bytes 2621456 | tf_op jit(solution)/shard_map/all_gather | solution.py:40
  452.8 13.3 %multiply_reduce_fusion.1 = (f32[160]{0:T(256)S(1)}, f32[160]{0:T(256)S(1)}, f32[512,160]{0,1:T(8,128)S(1)}) fusion(f32[512,160]{0,1:T(8,128)} %reduce-scatter.2.cloned.1.call-done, f32[512,4096]{1,0:T(8,128)} %all-reduce.3.cloned.1.call-done, f32[4096,160]{0,1:T(8,128)} %all-gather.6.cloned.1.call-done), kind=kOutput, calls=%fused_computation.7 | convolution fusion | flops 4026859264 | bytes 11666688 | tf_op jit(solution)/shard_map/dot_general | solution.py:39
  466.0 13.1 %all-reduce = (f32[160]{0:T(256)S(1)}, f32[160]{0:T(256)S(1)}) all-reduce(f32[160]{0:T(256)S(1)} %get-tuple-element.6, f32[160]{0:T(256)S(1)} %get-tuple-element.5), channel_id=1, replica_groups=mesh['silo'=4,'row'=8] {'row'}, use_global_device_ids=true, to_apply=%region_2.0 | all-reduce | flops 320 | bytes 2560 | tf_op jit(solution)/shard_map/psum | solution.py:44
  479.1 0.0 copy-done
  479.1 0.2 multiply_reduce_fusion
  479.3 12.0 %psum.38 = f32[160]{0:T(256)S(1)} all-reduce(f32[160]{0:T(256)S(1)} %multiply_reduce_fusion), channel_id=1, replica_groups=mesh['silo'=4,'row'=8] {'row'}, use_global_device_ids=true, to_apply=%region_8.0 | all-reduce | flops 160 | bytes 1280 | tf_op jit(solution)/shard_map/psum | solution.py:44
  491.4 0.9 multiply_add_fusion
  492.2 0.0 all-gather.8.cloned.1.call-update
  492.3 30.1 %all-gather.8.cloned.1.call-done = f32[4096,160]{0,1:T(8,128)} async-done(((f32[512,160]{0,1:T(8,128)}), f32[4096,160]{0,1:T(8,128)}) %all-gather.8.cloned.1.call-update) | async-done | bytes 2621456 | tf_op jit(solution)/shard_map/all_gather | solution.py:40
  522.4 13.2 %fusion = f32[160]{0:T(256)S(1)} fusion(f32[512,160]{0,1:T(8,128)} %multiply_add_fusion, f32[512,4096]{1,0:T(8,128)} %all-reduce.3.cloned.1.call-done, f32[4096,160]{0,1:T(8,128)} %all-gather.8.cloned.1.call-done), kind=kOutput, calls=%fused_computation.2 | convolution fusion | flops 4026695680 | bytes 11338368 | tf_op jit(solution)/shard_map/dot_general | solution.py:39
  535.7 13.1 %psum.39 = f32[160]{0:T(256)S(1)} all-reduce(f32[160]{0:T(256)S(1)} %fusion), channel_id=1, replica_groups=mesh['silo'=4,'row'=8] {'row'}, use_global_device_ids=true, to_apply=%region_10.0 | all-reduce | flops 160 | bytes 1280 | tf_op jit(solution)/shard_map/psum | solution.py:47
  548.7 0.0 copy-done.1
  548.8 0.1 add_bitcast_fusion
  548.9 10.9 %all_to_all.19 = f32[8,20,512]{2,1,0:T(8,128)S(1)} all-to-all(f32[8,20,512]{2,1,0:T(8,128)S(1)} %all_to_all.14), channel_id=1, replica_groups=mesh['silo'=4,'row'=8] {'row'}, dimensions={0} | all-to-all | bytes 655360 | tf_op jit(solution)/shard_map/all_to_all | solution.py:51
  559.8 0.2 copy.7
  560.0 1.0 copy.8
  (6 shorter events, 0.1 us)
Async XLA Ops:
  6.5 70.6 %all-gather.4.cloned.1.call-start = ((), (), s32[]{:S(2)}) async-start(), calls=%async_computation.2 | async-start | bytes 11796480 | tf_op jit(solution)/shard_map/all_gather | solution.py:32
  9.0 121.0 %reduce-scatter.2.cloned.1.call-start = ((), (), s32[]{:S(2)}) async-start(), calls=%async_computation.3 | async-start | bytes 1638400 | tf_op jit(solution)/shard_map/reduce_scatter | solution.py:36
  98.5 323.5 %all-reduce.3.cloned.1.call-start = ((), (), s32[]{:S(2)}) async-start(), calls=%async_computation.4 | async-start | bytes 16777216 | tf_op jit(solution)/shard_map/psum | solution.py:35
  110.1 342.7 %all-gather.6.cloned.1.call-start = ((), (), s32[]{:S(2)}) async-start(), calls=%async_computation.5 | async-start | bytes 2949120 | tf_op jit(solution)/shard_map/all_gather | solution.py:40
  130.0 349.2 %copy-start = (f32[512,160]{0,1:T(8,128)S(1)}, f32[512,160]{0,1:T(8,128)}, u32[]{:S(2)}) copy-start(f32[512,160]{0,1:T(8,128)} %reduce-scatter.2.cloned.1.call-done) | copy-start | bytes 983044
  130.0 392.4 %all-gather.8.cloned.1.call-start = ((), (), s32[]{:S(2)}) async-start(), calls=%async_computation.6 | async-start | bytes 2949120 | tf_op jit(solution)/shard_map/all_gather | solution.py:40
  492.2 56.5 %copy-start.1 = (f32[512,160]{0,1:T(8,128)S(1)}, f32[512,160]{0,1:T(8,128)}, u32[]{:S(2)}) copy-start(f32[512,160]{0,1:T(8,128)} %multiply_add_fusion) | copy-start | bytes 983044
Sparse Core Ops, SparseCore 0:
  9.2 67.8 all-gather.3
  98.6 31.3 reduce-scatter.1
  132.5 289.4 all-reduce.2
  423.8 28.9 all-gather.5
  492.4 29.9 all-gather.7
where the time goes:
time: 568 us
  waiting for transfers between devices  441 us (78%)
  blocking collectives  49 us (9%)
  matrix products  47.8 us (8%)
  between operations  13.2 us (2%)
  other arithmetic  12.8 us (2%)
    psum x1, waiting for transfers between devices, local(): operator = lax.psum(partial_op, 'silo')  292 us
    all_gather x1, waiting for transfers between devices, local(): lax.all_gather(silo_weights, 'row', axis=1, tiled=True).astype(jnp.float32)  68.1 us
    all_gather x2, waiting for transfers between devices, apply_cols(): lax.all_gather(direction, 'row', axis=0, tiled=True)  60.9 us
    dot_general x2, matrix products, apply_cols(): jnp.dot(operator, lax.all_gather(direction, 'row', axis=0, tiled=True), p...  26.5 us
    psum x2, blocking collectives, squares_cols(): return lax.psum(values, 'row')  25.1 us
    dot_general x1, matrix products, local(): jnp.einsum('srk,skc->rc', silo_grams, lax.all_gather(silo_weights, 'row',...  21.3 us
    reduce_scatter x1, waiting for transfers between devices, local(): lax.psum_scatter(partial_rhs, 'silo', scatter_dimension=1, tiled=True)  19.8 us
    psum x1, blocking collectives, curv_values(): return lax.psum(values, 'row')  13.1 us
  transfers between devices with their start and end apart: 5, of which 5 were waited for; matrix products, arithmetic and copies ran while one was open for 2% of the time, Pallas kernels for 0%

commit v1 on v0

--- a/solution.py
+++ b/solution.py
@@ -25,6 +25,11 @@
 
 
 def local(silo_grams, silo_weights):
+
+    def balance_cards(my_data, device_axis):
+        carry_in = lax.all_gather(my_data, device_axis)
+        return jnp.sum(carry_in, axis=0)
+
     partial_op = jnp.sum(silo_grams, axis=0)
     partial_rhs = jnp.einsum(
         "srk,skc->rc",
@@ -32,7 +37,7 @@
         lax.all_gather(silo_weights, "row", axis=1, tiled=True).astype(jnp.float32),
         precision=full_precision,
     )
-    operator = lax.psum(partial_op, "silo")
+    operator = balance_cards(partial_op, "silo")
     right_side = lax.psum_scatter(partial_rhs, "silo", scatter_dimension=1, tiled=True)
 
     def apply_cols(direction):

time: 568 us -> 835 us (1.47)
  waiting for transfers between devices: 441 us -> 694 us
  other arithmetic: 12.8 us -> 28.6 us
    all_gather x0 -> x1, waiting for transfers between devices: none -> 562 us  [balance_cards(): carry_in = lax.all_gather(my_data, device_axis)]
    psum x1 -> x0, waiting for transfers between devices: 292 us -> none  [local(): operator = lax.psum(partial_op, 'silo')]
    all_gather x2, waiting for transfers between devices: 60.9 us -> 44.3 us  [apply_cols(): lax.all_gather(direction, 'row', axis=0, tiled=True)]
    reduce_sum x0 -> x1, other arithmetic: none -> 15.8 us  [balance_cards(): return jnp.sum(carry_in, axis=0)]
  transfers between devices with their start and end apart: 5 -> 5, of which waited for: 5 -> 5; matrix products, arithmetic and copies ran while one was open for 2% -> 3% of each run, Pallas kernels for 0% -> 0%
where the time goes in v1:
time: 835 us
  waiting for transfers between devices  694 us (83%)
  blocking collectives  49 us (6%)
  matrix products  46.7 us (6%)
  other arithmetic  28.6 us (3%)
  between operations  13.2 us (2%)
    all_gather x1, waiting for transfers between devices, balance_cards(): carry_in = lax.all_gather(my_data, device_axis)  562 us
    all_gather x1, waiting for transfers between devices, local(): lax.all_gather(silo_weights, 'row', axis=1, tiled=True).astype(jnp.float32)  68.1 us
    all_gather x2, waiting for transfers between devices, apply_cols(): lax.all_gather(direction, 'row', axis=0, tiled=True)  44.3 us
    dot_general x2, matrix products, apply_cols(): jnp.dot(operator, lax.all_gather(direction, 'row', axis=0, tiled=True), p...  25.4 us
    psum x2, blocking collectives, squares_cols(): return lax.psum(values, 'row')  25.1 us
    dot_general x1, matrix products, local(): jnp.einsum('srk,skc->rc', silo_grams, lax.all_gather(silo_weights, 'row',...  21.3 us
    reduce_scatter x1, waiting for transfers between devices, local(): lax.psum_scatter(partial_rhs, 'silo', scatter_dimension=1, tiled=True)  19.8 us
  transfers between devices with their start and end apart: 5, of which 5 were waited for; matrix products, arithmetic and copies ran while one was open for 3% of the time, Pallas kernels for 0%

profile of v1, /device:TPU:0, one launch (start us, length us, event | category | flops | bytes accessed | tf_op | source)
XLA Modules:
  0.0 835.2 jit_solution(229290111698581191)
XLA Ops:
  6.5 0.0 all-gather.6.cloned.1.call-start
  6.5 2.4 copy.8
  9.0 0.0 all-gather.6.cloned.1.call-update
  9.0 0.0 reduce-scatter.2.cloned.1.call-start
  9.0 68.1 %all-gather.6.cloned.1.call-done = bf16[2,4096,640]{1,2,0:T(8,128)(2,1)} async-done(((bf16[2,512,640]{1,2,0:T(8,128)(2,1)}), bf16[2,4096,640]{1,2,0:T(8,128)(2,1)}) %all-gather.6.cloned.1.call-update) | async-done | bytes 10485776 | tf_op jit(solution)/shard_map/all_gather | solution.py:37
  77.1 21.3 %convolution_bitcast_fusion = f32[512,640]{0,1:T(8,128)} fusion(f32[2,512,4096]{2,1,0:T(8,128)} %param.2, bf16[2,4096,640]{1,2,0:T(8,128)(2,1)} %all-gather.6.cloned.1.call-done), kind=kOutput, calls=%fused_computation | convolution fusion | flops 32212254720 | bytes 28573696 | tf_op jit(solution)/shard_map/srk,skc->rc/dot_general | solution.py:34
  98.5 0.0 reduce-scatter.2.cloned.1.call-update
  98.5 0.0 all-gather.12.cloned.1.call-start
  98.5 11.5 %reduce_sum.55 = f32[512,4096]{1,0:T(8,128)} reduce(f32[2,512,4096]{2,1,0:T(8,128)} %param.2, f32[]{:T(128)} %constant.0.clone.1), dimensions={0}, to_apply=%region_3.0 | reduce | flops 2097152 | bytes 25165828 | tf_op jit(solution)/shard_map/reduce_sum | solution.py:33
  110.1 0.0 all-gather.12.cloned.1.call-update
  110.1 0.0 all-gather.8.cloned.1.call-start
  110.1 19.8 %reduce-scatter.2.cloned.1.call-done = f32[512,160]{0,1:T(8,128)} async-done(((f32[512,640]{0,1:T(8,128)}), f32[512,160]{0,1:T(8,128)}) %reduce-scatter.2.cloned.1.call-update) | async-done | bytes 327696 | tf_op jit(solution)/shard_map/reduce_scatter | solution.py:41
  130.0 0.0 all-gather.8.cloned.1.call-update
  130.0 0.0 all-gather.10.cloned.1.call-start
  130.1 561.6 %all-gather.12.cloned.1.call-done = f32[2048,4096]{1,0:T(8,128)} async-done(((f32[512,4096]{1,0:T(8,128)}), f32[2048,4096]{1,0:T(8,128)}) %all-gather.12.cloned.1.call-update) | async-done | bytes 33554448 | tf_op jit(solution)/shard_map/all_gather | solution.py:30
  691.7 15.8 %reduce_sum.56 = f32[512,4096]{1,0:T(8,128)} reduce(f32[4,512,4096]{2,1,0:T(8,128)} %bitcast.15, f32[]{:T(128)} %constant.0.clone.1), dimensions={0}, to_apply=%region_4.0 | reduce | flops 6291456 | bytes 41943044 | tf_op jit(solution)/shard_map/reduce_sum | solution.py:31
  707.5 14.1 %all-gather.8.cloned.1.call-done = f32[4096,160]{0,1:T(8,128)} async-done(((f32[512,160]{0,1:T(8,128)}), f32[4096,160]{0,1:T(8,128)}) %all-gather.8.cloned.1.call-update) | async-done | bytes 2621456 | tf_op jit(solution)/shard_map/all_gather | solution.py:45
  721.6 0.0 copy-done
  721.6 12.1 %multiply_reduce_fusion.1 = (f32[160]{0:T(256)S(1)}, f32[160]{0:T(256)S(1)}, f32[512,160]{0,1:T(8,128)S(1)}) fusion(f32[512,160]{0,1:T(8,128)S(1)} %copy-done, f32[512,4096]{1,0:T(8,128)} %reduce_sum.56, f32[4096,160]{0,1:T(8,128)} %all-gather.8.cloned.1.call-done), kind=kOutput, calls=%fused_computation.7 | convolution fusion | flops 4026859264 | bytes 11666688 | tf_op jit(solution)/shard_map/dot_general | solution.py:44
  733.8 13.1 %all-reduce = (f32[160]{0:T(256)S(1)}, f32[160]{0:T(256)S(1)}) all-reduce(f32[160]{0:T(256)S(1)} %get-tuple-element.6, f32[160]{0:T(256)S(1)} %get-tuple-element.5), channel_id=1, replica_groups=mesh['silo'=4,'row'=8] {'row'}, use_global_device_ids=true, to_apply=%region_2.0 | all-reduce | flops 320 | bytes 2560 | tf_op jit(solution)/shard_map/psum | solution.py:49
  746.9 0.2 multiply_reduce_fusion
  747.1 12.0 %psum.30 = f32[160]{0:T(256)S(1)} all-reduce(f32[160]{0:T(256)S(1)} %multiply_reduce_fusion), channel_id=1, replica_groups=mesh['silo'=4,'row'=8] {'row'}, use_global_device_ids=true, to_apply=%region_8.0 | all-reduce | flops 160 | bytes 1280 | tf_op jit(solution)/shard_map/psum | solution.py:49
  759.0 0.9 multiply_add_fusion
  759.9 0.0 all-gather.10.cloned.1.call-update
  759.9 30.1 %all-gather.10.cloned.1.call-done = f32[4096,160]{0,1:T(8,128)} async-done(((f32[512,160]{0,1:T(8,128)}), f32[4096,160]{0,1:T(8,128)}) %all-gather.10.cloned.1.call-update) | async-done | bytes 2621456 | tf_op jit(solution)/shard_map/all_gather | solution.py:45
  790.1 13.2 %fusion = f32[160]{0:T(256)S(1)} fusion(f32[512,160]{0,1:T(8,128)} %multiply_add_fusion, f32[512,4096]{1,0:T(8,128)} %reduce_sum.56, f32[4096,160]{0,1:T(8,128)} %all-gather.10.cloned.1.call-done), kind=kOutput, calls=%fused_computation.2 | convolution fusion | flops 4026695680 | bytes 11338368 | tf_op jit(solution)/shard_map/dot_general | solution.py:44
  803.3 13.1 %psum.31 = f32[160]{0:T(256)S(1)} all-reduce(f32[160]{0:T(256)S(1)} %fusion), channel_id=1, replica_groups=mesh['silo'=4,'row'=8] {'row'}, use_global_device_ids=true, to_apply=%region_10.0 | all-reduce | flops 160 | bytes 1280 | tf_op jit(solution)/shard_map/psum | solution.py:52
  816.4 0.0 copy-done.1
  816.4 0.1 add_bitcast_fusion
  816.6 10.9 %all_to_all.19 = f32[8,20,512]{2,1,0:T(8,128)S(1)} all-to-all(f32[8,20,512]{2,1,0:T(8,128)S(1)} %all_to_all.14), channel_id=1, replica_groups=mesh['silo'=4,'row'=8] {'row'}, dimensions={0} | all-to-all | bytes 655360 | tf_op jit(solution)/shard_map/all_to_all | solution.py:56
  827.5 0.2 copy.9
  827.7 1.0 copy.10
  (7 shorter events, 0.1 us)
Async XLA Ops:
  6.5 70.6 %all-gather.6.cloned.1.call-start = ((), (), s32[]{:S(2)}) async-start(), calls=%async_computation.2 | async-start | bytes 11796480 | tf_op jit(solution)/shard_map/all_gather | solution.py:37
  9.0 121.0 %reduce-scatter.2.cloned.1.call-start = ((), (), s32[]{:S(2)}) async-start(), calls=%async_computation.3 | async-start | bytes 1638400 | tf_op jit(solution)/shard_map/reduce_scatter | solution.py:41
  98.5 593.2 %all-gather.12.cloned.1.call-start = ((), (), s32[]{:S(2)}) async-start(), calls=%async_computation.6 | async-start | bytes 41943040 | tf_op jit(solution)/shard_map/all_gather | solution.py:30
  110.1 611.5 %all-gather.8.cloned.1.call-start = ((), (), s32[]{:S(2)}) async-start(), calls=%async_computation.4 | async-start | bytes 2949120 | tf_op jit(solution)/shard_map/all_gather | solution.py:45
  130.0 660.1 %all-gather.10.cloned.1.call-start = ((), (), s32[]{:S(2)}) async-start(), calls=%async_computation.5 | async-start | bytes 2949120 | tf_op jit(solution)/shard_map/all_gather | solution.py:45
  691.7 30.0 %copy-start = (f32[512,160]{0,1:T(8,128)S(1)}, f32[512,160]{0,1:T(8,128)}, u32[]{:S(2)}) copy-start(f32[512,160]{0,1:T(8,128)} %reduce-scatter.2.cloned.1.call-done) | copy-start | bytes 983044
  759.9 56.5 %copy-start.1 = (f32[512,160]{0,1:T(8,128)S(1)}, f32[512,160]{0,1:T(8,128)}, u32[]{:S(2)}) copy-start(f32[512,160]{0,1:T(8,128)} %multiply_add_fusion) | copy-start | bytes 983044
Sparse Core Ops, SparseCore 0:
  9.2 67.8 all-gather.5
  98.6 31.3 reduce-scatter.1
  131.6 560.0 all-gather.11
  693.4 28.1 all-gather.7
  760.1 29.9 all-gather.9
